TPU v7x, 512 devices: a 8x2x16 block of a 8x8x16 slice. The times are simulated.
512 devices in a mesh: rep: 2 (over y), seq: 16 (over z), head: 8 (over x), sub: 2 (over core).
Axes of the slice: x: 8, y: 2, z: 16, core: 2. Of those that a mesh axis runs over, the one named last changes fastest.
The devices are a block of a 8x8x16 slice.
Arguments:
- tokens: bfloat16 [32, 4096], P(('rep', 'sub'), 'seq'), parts along dimension 0, may hold values from -260 to 260
- attn_gain: float32 [4096], P('seq'), may hold values from 0.1 to 1.9
- w_query: bfloat16 [4096, 4096], P('seq', 'head'), may hold values from -0.09375 to 0.09375
- key_projection_weight: bfloat16 [4096, 1024], P('seq', 'head'), may hold values from -0.375 to 0.375
- value_projection_weight: bfloat16 [4096, 1024], P('seq', 'head'), may hold values from -0.375 to 0.375
- w_attn_out: bfloat16 [4096, 4096], P('head', 'seq'), may hold values from -0.09375 to 0.09375
- cache_keys: bfloat16 [32, 8, 8192, 128], P(('rep', 'sub'), 'head', 'seq'), parts along dimension 0, may hold values from -2500 to 2500
- stored_value_cache: bfloat16 [32, 8, 8192, 128], P(('rep', 'sub'), 'head', 'seq'), parts along dimension 0, may hold values from -12 to 12
- lengths: int32 [32], P(('rep', 'sub')), parts along dimension 0, may hold values from 4096 to 8192
- positions: int32 [32], P(('rep', 'sub')), parts along dimension 0, may hold values from 0 to 8191
- mamba_gain: float32 [4096], replicated, may hold values from 0.1 to 1.9
- w_in: bfloat16 [2, 4096, 8192], P(None, None, ('seq', 'head')), may hold values from -0.09375 to 0.09375
- conv_weight: float32 [4, 8192], P(None, ('seq', 'head')), may hold values from -3 to 3
- conv_bias: float32 [8192], P(('seq', 'head')), may hold values from -0.5 to 0.5
- conv_state: float32 [32, 3, 8192], P(('rep', 'sub'), None, ('seq', 'head')), parts along dimension 0, may hold values from -6 to 6
- w_xproj: bfloat16 [8192, 288], P(('seq', 'head')), may hold values from -0.0625 to 0.0625
- w_dt: bfloat16 [256, 8192], P(None, ('seq', 'head')), may hold values from -0.375 to 0.375
- dt_bias: float32 [8192], P(('seq', 'head')), may hold values from -4 to 0
- a_log: float32 [16, 8192], P(None, ('seq', 'head')), may hold values from 0 to 2.77
- skip_gain: float32 [8192], P(('seq', 'head')), may hold values from 0.25 to 2
- ssm_state: float32 [32, 16, 8192], P(('rep', 'sub'), None, ('seq', 'head')), parts along dimension 0, may hold values from -6 to 6
- w_mamba_out: bfloat16 [8192, 4096], P(('seq', 'head')), may hold values from -0.25 to 0.25
Outputs:
- hidden_out: bfloat16 [32, 4096], P(('rep', 'sub'), 'seq'), parts along dimension 0
- new_state: float32 [32, 16, 8192], P(('rep', 'sub'), None, ('seq', 'head')), parts along dimension 0
There are 2 independent parts, one for each index of `rep`. A program takes and returns all parts, laid end to end along the dimension named above; an argument that names none is the same for every part. Nothing has to cross between parts.
Inputs may be any that keep to these rules, and one draw needn't show every extreme that they name: Cache positions p < lengths[b] hold sequence b's past keys and values; later positions are not attended.
All inputs are finite; a program needn't handle non-finite values.
Results may differ from a plain program's by a relative error of at most 0.015.
Values may be sent and summed in bfloat16 or wider, within the bound.
A program may use at most 64 MiB of HBM per device.

v0:
```python
import math
import jax
import jax.numpy as jnp
from jax import lax
from jax.sharding import PartitionSpec as P

norm_eps = 1e-05
masked_floor = -1e30
rope_base = 10000.0


def copy_for_each(value, axis):
    peers = lax.axis_size(axis)
    return lax.all_to_all(
        jnp.broadcast_to(value[None], (peers, *value.shape)), axis, 0, 0, tiled=True
    )


def taken_together(value, axis):
    everything = copy_for_each(value, axis)
    return jnp.sum(everything, axis=0)


def together(arrays, axis):
    line, at, done = (jnp.concatenate([a.reshape(-1) for a in arrays]), 0, [])
    subtotal = taken_together(line, axis)
    for a in arrays:
        done.append(subtotal[at : at + a.size].reshape(a.shape))
        at += a.size
    return tuple(done)


def gathered_once(value, axis):
    leaves = jax.tree.leaves(value)
    turns = sorted(range(len(leaves)), key=lambda k: -leaves[k].size)
    width = (1, *leaves[turns[0]].shape)[-1]
    lines = [
        jnp.pad(leaves[k].reshape(-1), (0, -leaves[k].size % width)).reshape(-1, width)
        for k in turns
    ]
    both, at, found = (copy_for_each(jnp.concatenate(lines), axis), 0, {})
    for k, line in zip(turns, lines):
        section = both[:, at : at + len(line)].reshape(len(both), -1)
        found[k] = section[:, : leaves[k].size].reshape(-1, *leaves[k].shape)
        at += len(line)
    numbers = iter(range(len(leaves)))
    return jax.tree.map(lambda _: found[next(numbers)], value)


def combined_pairwise(pieces, combine):
    while len(jax.tree.leaves(pieces)[0]) > 1:
        pieces = jax.vmap(combine)(
            *(jax.tree.map(lambda part: part[side::2], pieces) for side in (0, 1))
        )
    return jax.tree.map(lambda part: part[0], pieces)


def merged(value, axis, combine):
    pieces = gathered_once(value, axis)
    return combined_pairwise(pieces, combine)


def in_order(blocks, dim):
    blocks = jnp.moveaxis(blocks, 0, dim)
    dims = blocks.shape
    return blocks.reshape(*dims[:dim], dims[dim] * dims[dim + 1], *dims[dim + 2 :])


def collect(value, axis, dim):
    return in_order(copy_for_each(value, axis), dim)


def over_axes(value, axes):
    for axis in axes:
        value = lax.psum(value, axis)
    return value


def in_blocks(value, dim, peers):
    dims = value.shape
    blocks = value.reshape(*dims[:dim], peers, dims[dim] // peers, *dims[dim + 1 :])
    return jnp.moveaxis(blocks, dim, 0)


def sent_and_summed(value, axis, dim):
    peers = lax.axis_size(axis)
    blocks = lax.all_to_all(in_blocks(value, dim, peers), axis, 0, 0, tiled=True)
    return jnp.sum(blocks.astype(jnp.float32), axis=0)


def apply_rotary(vectors, positions):
    half_dim = vectors.shape[-1] // 2
    frequency = jnp.exp(
        -math.log(rope_base) * 2.0 * jnp.arange(half_dim, dtype=jnp.float32) / (2 * half_dim)
    )
    angles = positions.astype(jnp.float32)[:, None] * frequency[None, :]
    cosine = jnp.cos(angles)[:, None, :]
    sine_part = jnp.sin(angles)[:, None, :]
    first_half = vectors[..., :half_dim]
    second_half = vectors[..., half_dim:]
    return jnp.concatenate(
        [
            first_half * cosine - second_half * sine_part,
            second_half * cosine + first_half * sine_part,
        ],
        axis=-1,
    )


def join_partial(earlier, later):
    max_one, sum_one, acc_one = earlier
    max_two, sum_two, acc_two = later
    joined_max = jnp.maximum(max_one, max_two)
    factor_one = jnp.exp(max_one - joined_max)
    factor_two = jnp.exp(max_two - joined_max)
    return (
        joined_max,
        sum_one * factor_one + sum_two * factor_two,
        acc_one * factor_one[..., None] + acc_two * factor_two[..., None],
    )


def local(
    tokens,
    attn_gain,
    w_query,
    key_projection_weight,
    value_projection_weight,
    w_attn_out,
    cache_keys,
    stored_value_cache,
    lengths,
    positions,
    mamba_gain,
    w_in,
    conv_weight,
    conv_bias,
    conv_state,
    w_xproj,
    w_dt,
    dt_bias,
    a_log,
    skip_gain,
    ssm_state,
    w_mamba_out,
):
    batch_rows = tokens.shape[0]
    feature_cols = tokens.shape[1]
    head_dim = cache_keys.shape[3]
    kv_local = cache_keys.shape[1]
    ctx_local = cache_keys.shape[2]
    q_local = w_query.shape[1] // head_dim
    query_group_count = q_local // kv_local
    model_width = feature_cols * lax.axis_size("seq")
    token_float = tokens.astype(jnp.float32)
    lifted = (token_float * attn_gain[None, :]).astype(jnp.bfloat16)
    part_query = jnp.dot(lifted, w_query, preferred_element_type=jnp.float32)
    part_key = jnp.dot(lifted, key_projection_weight, preferred_element_type=jnp.float32)
    part_value = jnp.dot(lifted, value_projection_weight, preferred_element_type=jnp.float32)
    squares = jnp.sum(token_float * token_float, axis=1)
    part_query, part_key, part_value, sum_squares = together(
        (part_query, part_key, part_value, squares), "seq"
    )
    inv_rms = lax.rsqrt(sum_squares / model_width + norm_eps)
    query_vectors = apply_rotary(
        (part_query * inv_rms[:, None]).reshape(batch_rows, q_local, head_dim), positions
    ).astype(jnp.bfloat16)
    fresh_key_rows = apply_rotary(
        (part_key * inv_rms[:, None]).reshape(batch_rows, kv_local, head_dim), positions
    ).astype(jnp.bfloat16)
    fresh_value_rows = (
        (part_value * inv_rms[:, None]).reshape(batch_rows, kv_local, head_dim).astype(jnp.bfloat16)
    )
    grouped_queries = query_vectors.reshape(batch_rows, kv_local, query_group_count, head_dim)
    score_scale = head_dim ** (-0.5)
    scores = (
        jnp.einsum(
            "bhgd,bhtd->bhgt", grouped_queries, cache_keys, preferred_element_type=jnp.float32
        )
        * score_scale
    )
    slot_index = lax.axis_index("seq") * ctx_local + jnp.arange(ctx_local, dtype=jnp.int32)
    live_mask = slot_index[None, None, None, :] < lengths[:, None, None, None]
    local_max = jnp.max(jnp.where(live_mask, scores, masked_floor), axis=-1)
    weights = jnp.where(live_mask, jnp.exp(scores - local_max[..., None]), 0.0)
    local_sum = jnp.sum(weights, axis=-1)
    local_acc = jnp.einsum(
        "bhgt,bhtd->bhgd",
        weights.astype(jnp.bfloat16),
        stored_value_cache,
        preferred_element_type=jnp.float32,
    )
    merged_max, merged_sum, merged_acc = merged(
        (local_max, local_sum, local_acc), "seq", join_partial
    )
    score_new = (
        jnp.einsum(
            "bhgd,bhd->bhg", grouped_queries.astype(jnp.float32), fresh_key_rows.astype(jnp.float32)
        )
        * score_scale
    )
    row_max = jnp.maximum(merged_max, score_new)
    old_factor = jnp.exp(merged_max - row_max)
    new_weight = jnp.exp(score_new - row_max)
    total_weight = merged_sum * old_factor + new_weight
    attended = (
        merged_acc * old_factor[..., None]
        + new_weight[..., None] * fresh_value_rows.astype(jnp.float32)[:, :, None, :]
    )
    attn_rows = (
        (attended / total_weight[..., None])
        .reshape(batch_rows, q_local * head_dim)
        .astype(jnp.bfloat16)
    )
    out_part = jnp.dot(attn_rows, w_attn_out, preferred_element_type=jnp.float32)
    summed = taken_together(out_part, "head")
    mid_stream = (token_float + summed).astype(jnp.bfloat16)
    full_tokens = collect(mid_stream, "seq", 1)
    full_float = full_tokens.astype(jnp.float32)
    inv_rms_two = lax.rsqrt(jnp.mean(full_float * full_float, axis=1) + norm_eps)
    lifted_two = (full_float * inv_rms_two[:, None] * mamba_gain[None, :]).astype(jnp.bfloat16)
    inner = jnp.dot(lifted_two, w_in[0], preferred_element_type=jnp.float32)
    gate_branch = jnp.dot(lifted_two, w_in[1], preferred_element_type=jnp.float32)
    window = jnp.concatenate([conv_state, inner[:, None, :]], axis=1)
    mixed = jnp.sum(window * conv_weight[None, :, :], axis=1) + conv_bias[None, :]
    activated = jax.nn.silu(mixed)
    proj_part = jnp.dot(activated.astype(jnp.bfloat16), w_xproj, preferred_element_type=jnp.float32)
    projected = over_axes(proj_part, ("seq", "head"))
    rank_width = w_dt.shape[0]
    state_width = ssm_state.shape[1]
    dt_low = projected[:, :rank_width].astype(jnp.bfloat16)
    input_map = projected[:, rank_width : rank_width + state_width]
    output_map = projected[:, rank_width + state_width :]
    step_size = jax.nn.softplus(
        jnp.dot(dt_low, w_dt, preferred_element_type=jnp.float32) + dt_bias[None, :]
    )
    decay = jnp.exp(step_size[:, None, :] * (-jnp.exp(a_log))[None, :, :])
    new_state = decay * ssm_state + (step_size * activated)[:, None, :] * input_map[:, :, None]
    readout = jnp.sum(output_map[:, :, None] * new_state, axis=1) + skip_gain[None, :] * activated
    gated = (readout * jax.nn.silu(gate_branch)).astype(jnp.bfloat16)
    mamba_part = jnp.dot(gated, w_mamba_out, preferred_element_type=jnp.float32)
    share = sent_and_summed(mamba_part.astype(jnp.bfloat16), "seq", 1)
    share = taken_together(share, "head")
    hidden_out = (mid_stream.astype(jnp.float32) + share).astype(jnp.bfloat16)
    return (hidden_out, new_state)


def solution(mesh):
    in_specs = (
        P(("rep", "sub"), "seq"),
        P("seq"),
        P("seq", "head"),
        P("seq", "head"),
        P("seq", "head"),
        P("head", "seq"),
        P(("rep", "sub"), "head", "seq", None),
        P(("rep", "sub"), "head", "seq", None),
        P(("rep", "sub")),
        P(("rep", "sub")),
        P(),
        P(None, None, ("seq", "head")),
        P(None, ("seq", "head")),
        P(("seq", "head")),
        P(("rep", "sub"), None, ("seq", "head")),
        P(("seq", "head"), None),
        P(None, ("seq", "head")),
        P(("seq", "head")),
        P(None, ("seq", "head")),
        P(("seq", "head")),
        P(("rep", "sub"), None, ("seq", "head")),
        P(("seq", "head"), None),
    )
    out_specs = (P(("rep", "sub"), "seq"), P(("rep", "sub"), None, ("seq", "head")))
    return jax.shard_map(local, mesh=mesh, in_specs=in_specs, out_specs=out_specs, check_vma=False)
```

profile of v0, /device:TPU:80, one launch (start us, length us, event | category | flops | bytes accessed | tf_op | source)
XLA Modules:
  0.0 256.3 jit_solution(7575589292232890467)
XLA Ops:
  0.7 0.9 fusion.26
  1.6 1.1 convolution_bitcast_fusion
  2.8 0.1 convolution_bitcast_fusion.1
  2.9 0.7 copy-done.6
  3.6 0.1 convolution_bitcast_fusion.2
  3.7 1.0 broadcast_in_dim.31
  4.7 43.8 %all-to-all-start = ((f32[16,1,6152]{2,1,0:T(1,128)}), f32[16,1,6152]{2,1,0:T(1,128)S(1)}, u32[]{:S(2)}, u32[]{:S(2)}) async-start(f32[16,1,6152]{2,1,0:T(1,128)} %broadcast_in_dim.31), calls=%async_computation | async-start | bytes 802816 | tf_op jit(solution)/shard_map/all_to_all | solution.py:14
  48.8 23.8 %all-to-all-done = f32[16,1,6152]{2,1,0:T(1,128)S(1)} async-done(((f32[16,1,6152]{2,1,0:T(1,128)}), f32[16,1,6152]{2,1,0:T(1,128)S(1)}, u32[]{:S(2)}, u32[]{:S(2)}) %all-to-all-start) | async-done | bytes 393760 | tf_op jit(solution)/shard_map/all_to_all | solution.py:14
  72.6 0.3 reduce_sum.82
  73.0 0.5 select_reduce_fusion
  73.6 0.2 fusion.11
  73.9 0.3 fusion
  74.2 0.8 broadcast_in_dim.34
  75.0 6.1 %all-to-all-start.1 = ((f32[16,34,128]{2,1,0:T(8,128)}), f32[16,34,128]{2,1,0:T(8,128)S(1)}, u32[]{:S(2)}, u32[]{:S(2)}) async-start(f32[16,34,128]{2,1,0:T(8,128)} %broadcast_in_dim.34), calls=%async_computation.1 | async-start | bytes 655360 | tf_op jit(solution)/shard_map/all_to_all | solution.py:14
  81.4 0.2 fusion.51
  81.7 19.9 %all-to-all-done.1 = f32[16,34,128]{2,1,0:T(8,128)S(1)} async-done(((f32[16,34,128]{2,1,0:T(8,128)}), f32[16,34,128]{2,1,0:T(8,128)S(1)}, u32[]{:S(2)}, u32[]{:S(2)}) %all-to-all-start.1) | async-done | bytes 278560 | tf_op jit(solution)/shard_map/all_to_all | solution.py:14
  101.8 0.1 slice.142
  102.4 0.2 copy.147
  102.5 0.2 slice.138
  102.7 0.2 slice.143
  103.4 0.1 multiply_add_fusion
  103.6 0.2 slice.144
  103.8 0.2 slice.147
  104.3 0.1 multiply_add_fusion.2
  104.5 0.2 slice.148
  104.7 0.2 slice.151
  105.4 0.1 multiply_add_fusion.3
  105.5 0.2 fusion.22
  105.7 0.2 fusion.23
  105.9 15.5 %all_to_all.31 = f32[8,8,256]{2,1,0:T(8,128)S(1)} all-to-all(f32[8,8,256]{2,1,0:T(8,128)S(1)} %broadcast_in_dim.35), channel_id=1, replica_groups=mesh['rep'=2,'seq'=16,'head'=8,'sub'=2] {'head'}, dimensions={0} | all-to-all | bytes 131072 | tf_op jit(solution)/shard_map/all_to_all | solution.py:14
  121.4 0.6 broadcast_in_dim.36
  122.0 6.5 %all-to-all-start.3 = ((bf16[16,8,256]{2,1,0:T(8,128)(2,1)}), bf16[16,8,256]{2,1,0:T(8,128)(2,1)S(1)}, u32[]{:S(2)}, u32[]{:S(2)}) async-start(bf16[16,8,256]{2,1,0:T(8,128)(2,1)} %broadcast_in_dim.36), calls=%async_computation.3 | async-start | bytes 131072 | tf_op jit(solution)/shard_map/all_to_all | solution.py:14
  128.6 0.7 copy-done.13
  129.3 12.0 %all-to-all-done.3 = bf16[16,8,256]{2,1,0:T(8,128)(2,1)S(1)} async-done(((bf16[16,8,256]{2,1,0:T(8,128)(2,1)}), bf16[16,8,256]{2,1,0:T(8,128)(2,1)S(1)}, u32[]{:S(2)}, u32[]{:S(2)}) %all-to-all-start.3) | async-done | bytes 65568 | tf_op jit(solution)/shard_map/all_to_all | solution.py:14
  141.2 0.1 fusion.8
  141.5 0.2 convolution_bitcast_fusion.3
  141.8 0.5 copy-done.11
  142.4 0.5 copy-done.14
  142.9 0.1 fusion.64
  143.0 54.0 %psum.14 = f32[8,288]{1,0:T(8,128)S(1)} all-reduce(f32[8,288]{1,0:T(8,128)S(1)} %fusion.64), channel_id=1, replica_groups=mesh['rep'=2,'seq'=16,'head'=8,'sub'=2] {'seq'}, use_global_device_ids=true, to_apply=%region_7.8 | all-reduce | flops 2304 | bytes 18432 | tf_op jit(solution)/shard_map/psum | solution.py:75
  197.1 27.5 %psum.15 = f32[8,288]{1,0:T(8,128)S(1)} all-reduce(f32[8,288]{1,0:T(8,128)S(1)} %psum.14), channel_id=1, replica_groups=mesh['rep'=2,'seq'=16,'head'=8,'sub'=2] {'head'}, use_global_device_ids=true, to_apply=%region_8.9 | all-reduce | flops 2304 | bytes 18432 | tf_op jit(solution)/shard_map/psum | solution.py:75
  224.6 0.1 fusion.79
  224.8 0.7 multiply_reduce_fusion
  225.5 0.7 copy-done.17
  226.2 0.6 convolution_convert_fusion
  226.7 17.0 %all_to_all.32 = bf16[16,8,256]{2,1,0:T(8,128)(2,1)S(1)} all-to-all(bf16[16,8,256]{2,1,0:T(8,128)(2,1)S(1)} %bitcast.133), channel_id=1, replica_groups=mesh['rep'=2,'seq'=16,'head'=8,'sub'=2] {'seq'}, dimensions={0} | all-to-all | bytes 131072 | tf_op jit(solution)/shard_map/all_to_all | solution.py:87
  243.7 11.9 %all_to_all.33 = f32[8,8,256]{2,1,0:T(8,128)S(1)} all-to-all(f32[8,8,256]{2,1,0:T(8,128)S(1)} %broadcast_in_dim.38), channel_id=1, replica_groups=mesh['rep'=2,'seq'=16,'head'=8,'sub'=2] {'head'}, dimensions={0} | all-to-all | bytes 131072 | tf_op jit(solution)/shard_map/all_to_all | solution.py:14
  255.7 0.6 add_convert_fusion.1
  (99 shorter events, 3.2 us)
Async XLA Ops:
  0.6 72.4 %copy-start = (bf16[8,1,512,128]{3,2,1,0:T(8,128)(2,1)S(1)}, bf16[8,1,512,128]{3,2,1,0:T(8,128)(2,1)}, u32[]{:S(2)}) copy-start(bf16[8,1,512,128]{3,2,1,0:T(8,128)(2,1)} %param.28) | copy-start | bytes 3145732
  0.6 0.9 copy-start.4
  1.6 1.2 copy-start.5
  1.6 1.2 copy-start.12
  2.7 0.8 copy-start.6
  4.7 43.8 %copy-start.20 = (s32[8]{0:T(128)S(1)}, s32[8]{0:T(128)}, u32[]{:S(2)}) copy-start(s32[8]{0:T(128)} %param.31) | copy-start | bytes 100
  4.7 43.9 %copy-start.18 = (s32[8]{0:T(128)S(1)}, s32[8]{0:T(128)}, u32[]{:S(2)}) copy-start(s32[8]{0:T(128)} %param.30) | copy-start | bytes 100
  4.7 67.9 %all-to-all-start = ((f32[16,1,6152]{2,1,0:T(1,128)}), f32[16,1,6152]{2,1,0:T(1,128)S(1)}, u32[]{:S(2)}, u32[]{:S(2)}) async-start(f32[16,1,6152]{2,1,0:T(1,128)} %broadcast_in_dim.31), calls=%async_computation | async-start | bytes 802816 | tf_op jit(solution)/shard_map/all_to_all | solution.py:14
  48.5 25.4 %copy-start.1 = (bf16[8,1,512,128]{3,2,1,0:T(8,128)(2,1)S(1)}, bf16[8,1,512,128]{3,2,1,0:T(8,128)(2,1)}, u32[]{:S(2)}) copy-start(bf16[8,1,512,128]{3,2,1,0:T(8,128)(2,1)} %param.29) | copy-start | bytes 3145732
  75.0 26.6 %all-to-all-start.1 = ((f32[16,34,128]{2,1,0:T(8,128)}), f32[16,34,128]{2,1,0:T(8,128)S(1)}, u32[]{:S(2)}, u32[]{:S(2)}) async-start(f32[16,34,128]{2,1,0:T(8,128)} %broadcast_in_dim.34), calls=%async_computation.1 | async-start | bytes 655360 | tf_op jit(solution)/shard_map/all_to_all | solution.py:14
  103.6 2.1 copy-start.19
  103.8 37.7 %copy-start.2 = (bf16[2,4096,64]{1,2,0:T(8,128)(2,1)S(1)}, bf16[2,4096,64]{1,2,0:T(8,128)(2,1)}, u32[]{:S(2)}) copy-start(bf16[2,4096,64]{1,2,0:T(8,128)(2,1)} %param.33) | copy-start | bytes 3145732
  122.0 6.5 %copy-start.10 = (f32[4096]{0:T(1024)S(1)}, f32[4096]{0:T(1024)}, u32[]{:S(2)}) copy-start(f32[4096]{0:T(1024)} %param.32) | copy-start | bytes 49156
  122.0 19.2 %all-to-all-start.3 = ((bf16[16,8,256]{2,1,0:T(8,128)(2,1)}), bf16[16,8,256]{2,1,0:T(8,128)(2,1)S(1)}, u32[]{:S(2)}, u32[]{:S(2)}) async-start(bf16[16,8,256]{2,1,0:T(8,128)(2,1)} %broadcast_in_dim.36), calls=%async_computation.3 | async-start | bytes 131072 | tf_op jit(solution)/shard_map/all_to_all | solution.py:14
  128.6 0.7 copy-start.13
  141.4 84.1 %copy-start.3 = (bf16[64,4096]{1,0:T(8,128)(2,1)S(1)}, bf16[64,4096]{1,0:T(8,128)(2,1)}, u32[]{:S(2)}) copy-start(bf16[64,4096]{1,0:T(8,128)(2,1)} %param.43) | copy-start | bytes 1572868
  141.5 0.8 copy-start.11
  141.5 0.8 copy-start.15
  141.5 0.9 copy-start.8
  142.3 0.7 copy-start.14
  142.3 82.4 %copy-start.16 = (f32[64]{0:T(128)S(1)}, f32[64]{0:T(128)}, u32[]{:S(2)}) copy-start(f32[64]{0:T(128)} %param.39) | copy-start | bytes 772
  142.9 81.7 %copy-start.9 = (bf16[256,64]{0,1:T(8,128)(2,1)S(1)}, bf16[256,64]{0,1:T(8,128)(2,1)}, u32[]{:S(2)}) copy-start(bf16[256,64]{0,1:T(8,128)(2,1)} %param.38) | copy-start | bytes 98308
  143.0 81.7 %copy-start.7 = (f32[8,16,64]{2,1,0:T(8,128)S(1)}, f32[8,16,64]{2,1,0:T(8,128)}, u32[]{:S(2)}) copy-start(f32[8,16,64]{2,1,0:T(8,128)} %param.42) | copy-start | bytes 98308
  225.5 0.7 copy-start.17
where the time goes:
time: 257 us; the launch traced here: 256 us
  blocking collectives  126 us (49%)
  starting transfers between devices  56.5 us (22%)
  waiting for transfers between devices  55.7 us (22%)
  local copies, waits for them, and re-layouts  9.12 us (4%)
  other arithmetic  4.35 us (2%)
  matrix products  3.63 us (1%)
    psum x2, blocking collectives, over_axes(): value = lax.psum(value, axis)  81.5 us
    all_to_all x3, starting transfers between devices, copy_for_each(): lax.all_to_all(jnp.broadcast_to(value[None], (peers, *value.shape)), axis...  56.5 us
    all_to_all x3, waiting for transfers between devices, copy_for_each(): lax.all_to_all(jnp.broadcast_to(value[None], (peers, *value.shape)), axis...  55.7 us
    all_to_all x2, blocking collectives, copy_for_each(): lax.all_to_all(jnp.broadcast_to(value[None], (peers, *value.shape)), axis...  27.4 us
    all_to_all x1, blocking collectives, sent_and_summed(): lax.all_to_all(in_blocks(value, dim, peers), axis, 0, 0, tiled=True)  17 us
  transfers between devices with their start and end apart: 3, of which 3 were waited for; matrix products, arithmetic and copies ran while one was open for 0% of the time, Pallas kernels for 0%

commit v1 on v0

--- a/solution.py
+++ b/solution.py
@@ -72,7 +72,7 @@
 
 def over_axes(value, axes):
     for axis in axes:
-        value = lax.psum(value, axis)
+        value = jnp.sum(lax.all_gather(value, axis), axis=0)
     return value
 
 

time: 257 us -> 228 us (0.89)
  blocking collectives: 126 us -> 96.3 us
    psum x2 -> x0, blocking collectives: 81.5 us -> none  [over_axes(): value = lax.psum(value, axis)]
    all_gather x0 -> x2, blocking collectives: none -> 53 us  [over_axes(): value = jnp.sum(lax.all_gather(value, axis), axis=0)]
where the time goes in v1:
time: 228 us; the launch traced here: 227 us
  blocking collectives  96.3 us (42%)
  starting transfers between devices  56.5 us (25%)
  waiting for transfers between devices  55.7 us (24%)
  local copies, waits for them, and re-layouts  9.18 us (4%)
  other arithmetic  4.39 us (2%)
  matrix products  3.63 us (2%)
    all_to_all x3, starting transfers between devices, copy_for_each(): lax.all_to_all(jnp.broadcast_to(value[None], (peers, *value.shape)), axis...  56.5 us
    all_to_all x3, waiting for transfers between devices, copy_for_each(): lax.all_to_all(jnp.broadcast_to(value[None], (peers, *value.shape)), axis...  55.7 us
    all_gather x2, blocking collectives, over_axes(): value = jnp.sum(lax.all_gather(value, axis), axis=0)  53 us
    all_to_all x2, blocking collectives, copy_for_each(): lax.all_to_all(jnp.broadcast_to(value[None], (peers, *value.shape)), axis...  26.4 us
    all_to_all x1, blocking collectives, sent_and_summed(): lax.all_to_all(in_blocks(value, dim, peers), axis, 0, 0, tiled=True)  16.8 us
  transfers between devices with their start and end apart: 3, of which 3 were waited for; matrix products, arithmetic and copies ran while one was open for 0% of the time, Pallas kernels for 0%

profile of v1, /device:TPU:80, one launch (start us, length us, event | category | flops | bytes accessed | tf_op | source)
XLA Modules:
  0.0 226.8 jit_solution(343592398294317679)
XLA Ops:
  0.7 0.9 fusion.26
  1.6 1.1 convolution_bitcast_fusion
  2.8 0.1 convolution_bitcast_fusion.1
  2.9 0.7 copy-done.6
  3.6 0.1 convolution_bitcast_fusion.2
  3.7 1.0 broadcast_in_dim.31
  4.7 43.8 %all-to-all-start = ((f32[16,1,6152]{2,1,0:T(1,128)}), f32[16,1,6152]{2,1,0:T(1,128)S(1)}, u32[]{:S(2)}, u32[]{:S(2)}) async-start(f32[16,1,6152]{2,1,0:T(1,128)} %broadcast_in_dim.31), calls=%async_computation | async-start | bytes 802816 | tf_op jit(solution)/shard_map/all_to_all | solution.py:14
  48.8 23.8 %all-to-all-done = f32[16,1,6152]{2,1,0:T(1,128)S(1)} async-done(((f32[16,1,6152]{2,1,0:T(1,128)}), f32[16,1,6152]{2,1,0:T(1,128)S(1)}, u32[]{:S(2)}, u32[]{:S(2)}) %all-to-all-start) | async-done | bytes 393760 | tf_op jit(solution)/shard_map/all_to_all | solution.py:14
  72.6 0.3 reduce_sum.100
  73.0 0.5 select_reduce_fusion
  73.6 0.2 fusion.11
  73.9 0.3 fusion
  74.2 0.8 broadcast_in_dim.34
  75.0 6.1 %all-to-all-start.1 = ((f32[16,34,128]{2,1,0:T(8,128)}), f32[16,34,128]{2,1,0:T(8,128)S(1)}, u32[]{:S(2)}, u32[]{:S(2)}) async-start(f32[16,34,128]{2,1,0:T(8,128)} %broadcast_in_dim.34), calls=%async_computation.1 | async-start | bytes 655360 | tf_op jit(solution)/shard_map/all_to_all | solution.py:14
  81.4 0.2 fusion.51
  81.7 19.9 %all-to-all-done.1 = f32[16,34,128]{2,1,0:T(8,128)S(1)} async-done(((f32[16,34,128]{2,1,0:T(8,128)}), f32[16,34,128]{2,1,0:T(8,128)S(1)}, u32[]{:S(2)}, u32[]{:S(2)}) %all-to-all-start.1) | async-done | bytes 278560 | tf_op jit(solution)/shard_map/all_to_all | solution.py:14
  101.8 0.1 slice.142
  102.4 0.2 copy.147
  102.5 0.2 slice.138
  102.7 0.2 slice.143
  103.4 0.1 multiply_add_fusion
  103.6 0.2 slice.144
  103.8 0.2 slice.147
  104.3 0.1 multiply_add_fusion.2
  104.5 0.2 slice.148
  104.7 0.2 slice.151
  105.4 0.1 multiply_add_fusion.3
  105.5 0.2 fusion.22
  105.7 0.2 fusion.23
  105.9 15.5 %all_to_all.31 = f32[8,8,256]{2,1,0:T(8,128)S(1)} all-to-all(f32[8,8,256]{2,1,0:T(8,128)S(1)} %broadcast_in_dim.35), channel_id=1, replica_groups=mesh['rep'=2,'seq'=16,'head'=8,'sub'=2] {'head'}, dimensions={0} | all-to-all | bytes 131072 | tf_op jit(solution)/shard_map/all_to_all | solution.py:14
  121.4 0.6 broadcast_in_dim.36
  122.0 6.5 %all-to-all-start.3 = ((bf16[16,8,256]{2,1,0:T(8,128)(2,1)}), bf16[16,8,256]{2,1,0:T(8,128)(2,1)S(1)}, u32[]{:S(2)}, u32[]{:S(2)}) async-start(bf16[16,8,256]{2,1,0:T(8,128)(2,1)} %broadcast_in_dim.36), calls=%async_computation.3 | async-start | bytes 131072 | tf_op jit(solution)/shard_map/all_to_all | solution.py:14
  128.6 0.7 copy-done.13
  129.3 12.0 %all-to-all-done.3 = bf16[16,8,256]{2,1,0:T(8,128)(2,1)S(1)} async-done(((bf16[16,8,256]{2,1,0:T(8,128)(2,1)}), bf16[16,8,256]{2,1,0:T(8,128)(2,1)S(1)}, u32[]{:S(2)}, u32[]{:S(2)}) %all-to-all-start.3) | async-done | bytes 65568 | tf_op jit(solution)/shard_map/all_to_all | solution.py:14
  141.2 0.1 fusion.8
  141.5 0.2 convolution_bitcast_fusion.3
  141.8 0.4 copy-done.11
  142.3 0.1 fusion.64
  142.5 28.4 %all-gather = f32[128,288]{1,0:T(8,128)S(1)} all-gather(f32[8,288]{1,0:T(8,128)S(1)} %fusion.64), channel_id=2, replica_groups=mesh['rep'=2,'seq'=16,'head'=8,'sub'=2] {'seq'}, dimensions={0}, use_global_device_ids=true | all-gather | bytes 156672 | tf_op jit(solution)/shard_map/all_gather | solution.py:75
  170.9 24.7 %all-gather.1 = f32[64,288]{1,0:T(8,128)S(1)} all-gather(f32[8,288]{1,0:T(8,128)S(1)} %bitcast_reduce_fusion), channel_id=3, replica_groups=mesh['rep'=2,'seq'=16,'head'=8,'sub'=2] {'head'}, dimensions={0}, use_global_device_ids=true | all-gather | bytes 82944 | tf_op jit(solution)/shard_map/all_gather | solution.py:75
  195.6 0.7 copy-done.9
  196.3 0.1 fusion.79
  196.4 0.7 multiply_reduce_fusion
  197.2 0.7 copy-done.17
  197.8 0.6 convolution_convert_fusion
  198.4 16.8 %all_to_all.32 = bf16[16,8,256]{2,1,0:T(8,128)(2,1)S(1)} all-to-all(bf16[16,8,256]{2,1,0:T(8,128)(2,1)S(1)} %bitcast.137), channel_id=1, replica_groups=mesh['rep'=2,'seq'=16,'head'=8,'sub'=2] {'seq'}, dimensions={0} | all-to-all | bytes 131072 | tf_op jit(solution)/shard_map/all_to_all | solution.py:87
  215.2 10.9 %all_to_all.33 = f32[8,8,256]{2,1,0:T(8,128)S(1)} all-to-all(f32[8,8,256]{2,1,0:T(8,128)S(1)} %broadcast_in_dim.38), channel_id=1, replica_groups=mesh['rep'=2,'seq'=16,'head'=8,'sub'=2] {'head'}, dimensions={0} | all-to-all | bytes 131072 | tf_op jit(solution)/shard_map/all_to_all | solution.py:14
  226.2 0.6 add_convert_fusion.1
  (101 shorter events, 3.3 us)
Async XLA Ops:
  0.6 72.4 %copy-start = (bf16[8,1,512,128]{3,2,1,0:T(8,128)(2,1)S(1)}, bf16[8,1,512,128]{3,2,1,0:T(8,128)(2,1)}, u32[]{:S(2)}) copy-start(bf16[8,1,512,128]{3,2,1,0:T(8,128)(2,1)} %param.28) | copy-start | bytes 3145732
  0.6 0.9 copy-start.4
  1.6 1.2 copy-start.5
  1.6 1.2 copy-start.12
  2.7 0.8 copy-start.6
  4.7 43.8 %copy-start.20 = (s32[8]{0:T(128)S(1)}, s32[8]{0:T(128)}, u32[]{:S(2)}) copy-start(s32[8]{0:T(128)} %param.31) | copy-start | bytes 100
  4.7 43.9 %copy-start.18 = (s32[8]{0:T(128)S(1)}, s32[8]{0:T(128)}, u32[]{:S(2)}) copy-start(s32[8]{0:T(128)} %param.30) | copy-start | bytes 100
  4.7 67.9 %all-to-all-start = ((f32[16,1,6152]{2,1,0:T(1,128)}), f32[16,1,6152]{2,1,0:T(1,128)S(1)}, u32[]{:S(2)}, u32[]{:S(2)}) async-start(f32[16,1,6152]{2,1,0:T(1,128)} %broadcast_in_dim.31), calls=%async_computation | async-start | bytes 802816 | tf_op jit(solution)/shard_map/all_to_all | solution.py:14
  48.5 25.4 %copy-start.1 = (bf16[8,1,512,128]{3,2,1,0:T(8,128)(2,1)S(1)}, bf16[8,1,512,128]{3,2,1,0:T(8,128)(2,1)}, u32[]{:S(2)}) copy-start(bf16[8,1,512,128]{3,2,1,0:T(8,128)(2,1)} %param.29) | copy-start | bytes 3145732
  75.0 26.6 %all-to-all-start.1 = ((f32[16,34,128]{2,1,0:T(8,128)}), f32[16,34,128]{2,1,0:T(8,128)S(1)}, u32[]{:S(2)}, u32[]{:S(2)}) async-start(f32[16,34,128]{2,1,0:T(8,128)} %broadcast_in_dim.34), calls=%async_computation.1 | async-start | bytes 655360 | tf_op jit(solution)/shard_map/all_to_all | solution.py:14
  103.6 2.1 copy-start.19
  103.8 37.7 %copy-start.2 = (bf16[2,4096,64]{1,2,0:T(8,128)(2,1)S(1)}, bf16[2,4096,64]{1,2,0:T(8,128)(2,1)}, u32[]{:S(2)}) copy-start(bf16[2,4096,64]{1,2,0:T(8,128)(2,1)} %param.33) | copy-start | bytes 3145732
  122.0 6.5 %copy-start.10 = (f32[4096]{0:T(1024)S(1)}, f32[4096]{0:T(1024)}, u32[]{:S(2)}) copy-start(f32[4096]{0:T(1024)} %param.32) | copy-start | bytes 49156
  122.0 19.2 %all-to-all-start.3 = ((bf16[16,8,256]{2,1,0:T(8,128)(2,1)}), bf16[16,8,256]{2,1,0:T(8,128)(2,1)S(1)}, u32[]{:S(2)}, u32[]{:S(2)}) async-start(bf16[16,8,256]{2,1,0:T(8,128)(2,1)} %broadcast_in_dim.36), calls=%async_computation.3 | async-start | bytes 131072 | tf_op jit(solution)/shard_map/all_to_all | solution.py:14
  128.6 0.7 copy-start.13
  141.5 0.7 copy-start.11
  141.5 0.7 copy-start.15
  141.5 0.8 copy-start.8
  141.5 0.8 copy-start.14
  142.2 55.0 %copy-start.3 = (bf16[64,4096]{1,0:T(8,128)(2,1)S(1)}, bf16[64,4096]{1,0:T(8,128)(2,1)}, u32[]{:S(2)}) copy-start(bf16[64,4096]{1,0:T(8,128)(2,1)} %param.43) | copy-start | bytes 1572868
  170.9 24.8 %copy-start.16 = (f32[64]{0:T(128)S(1)}, f32[64]{0:T(128)}, u32[]{:S(2)}) copy-start(f32[64]{0:T(128)} %param.39) | copy-start | bytes 772
  195.5 0.8 copy-start.9
  195.5 0.9 copy-start.7
  197.2 0.7 copy-start.17
